TPU v7x, 32 devices: a whole 2x2x4 slice. The times are simulated.
32 devices in a mesh: seq: 4 (over y, x), fsdp: 8 (over z, core).
Axes of the slice: x: 2, y: 2, z: 4, core: 2. Of those that a mesh axis runs over, the one named last changes fastest.
Arguments:
- tokens: bfloat16 [8, 512, 8192], P('fsdp', 'seq'), may hold values from -6 to 6
- norm_gain: float32 [8192], replicated, may hold values from 0.3 to 3
- w_query: bfloat16 [8192, 4096], P(('seq', 'fsdp')), may hold values from -1 to 1
- key_weight: bfloat16 [8192, 512], P(('seq', 'fsdp')), may hold values from -1 to 1
- value_weight: bfloat16 [8192, 512], P(('seq', 'fsdp')), may hold values from -0.0625 to 0.0625
- w_out: bfloat16 [4096, 8192], P(None, ('seq', 'fsdp')), may hold values from -0.09375 to 0.09375
Outputs:
- result: float32 [8, 512, 8192], P('fsdp', 'seq')
All inputs are finite; a program needn't handle non-finite values.
Results may differ from a plain program's by a relative error of at most 0.04.
Values may be sent and summed in bfloat16 or wider, within the bound.
A program may use at most 128 MiB of HBM per device.

v0:
```python
import jax
import jax.numpy as jnp
from jax import lax
from jax.sharding import PartitionSpec as P

HEAD_SIZE = 128


def body(tokens, norm_gain, w_query, key_weight, value_weight, w_out):
    floats = tokens[0].astype(jnp.float32)
    mean_square = jnp.mean(floats * floats, axis=-1, keepdims=True)
    normed_input = (floats * lax.rsqrt(mean_square + 1e-05) * norm_gain).astype(jnp.bfloat16)
    spread = lax.all_to_all(normed_input[None], "seq", split_axis=2, concat_axis=1, tiled=True)[0]
    seq_length = spread.shape[0]
    group_size = lax.axis_size("seq")
    device_index = lax.axis_index("seq")
    query_heads = w_query.shape[1] // HEAD_SIZE
    key_heads = key_weight.shape[1] // HEAD_SIZE
    group_width = query_heads // key_heads
    local_heads = query_heads // group_size
    portions = (
        lax.all_gather(w_query, "fsdp", axis=0, tiled=True),
        lax.all_gather(key_weight, "fsdp", axis=0, tiled=True),
        lax.all_gather(value_weight, "fsdp", axis=0, tiled=True),
    )
    query_part, key_part, value_part = tuple(
        (jnp.dot(spread, portion, preferred_element_type=jnp.float32) for portion in portions)
    )
    query_sum = lax.psum_scatter(
        query_part.astype(jnp.bfloat16), "seq", scatter_dimension=1, tiled=True
    )
    key_all, value_all = (
        lax.psum(key_part.astype(jnp.bfloat16), "seq").astype(jnp.float32),
        lax.psum(value_part.astype(jnp.bfloat16), "seq").astype(jnp.float32),
    )
    offset = device_index * local_heads // group_width * HEAD_SIZE
    key_rows = lax.dynamic_slice_in_dim(key_all, offset, HEAD_SIZE, 1).astype(jnp.bfloat16)
    value_rows = lax.dynamic_slice_in_dim(value_all, offset, HEAD_SIZE, 1).astype(jnp.bfloat16)
    queries = jnp.transpose(query_sum.reshape(seq_length, local_heads, HEAD_SIZE), (1, 0, 2))
    scale = HEAD_SIZE ** (-0.5)
    row_ids = lax.broadcasted_iota(jnp.int32, (seq_length, seq_length), 0)
    col_ids = lax.broadcasted_iota(jnp.int32, (seq_length, seq_length), 1)
    causal = row_ids >= col_ids

    def one_head(query_head):
        scores = (
            jnp.einsum("qd,kd->qk", query_head, key_rows, preferred_element_type=jnp.float32)
            * scale
        )
        scores = jnp.where(causal, scores, jnp.float32(-1e30))
        top = jnp.max(scores, axis=-1, keepdims=True)
        weights = jnp.exp(scores - top)
        probs = (weights / jnp.sum(weights, axis=-1, keepdims=True)).astype(jnp.bfloat16)
        return jnp.dot(probs, value_rows, preferred_element_type=jnp.float32).astype(jnp.bfloat16)

    attended = lax.map(one_head, queries)
    heads_out = jnp.transpose(attended, (1, 0, 2)).reshape(seq_length, local_heads * HEAD_SIZE)
    out_columns = lax.all_gather(w_out, "fsdp", axis=1, tiled=True)
    mixed = jnp.dot(
        lax.all_gather(heads_out, "seq", axis=1, tiled=True),
        out_columns,
        preferred_element_type=jnp.float32,
    )
    branch = mixed.astype(jnp.bfloat16)
    returned = lax.all_to_all(branch[None], "seq", split_axis=1, concat_axis=2, tiled=True)
    return tokens.astype(jnp.float32) + returned.astype(jnp.float32)


def solution(mesh):
    placed = (
        P("fsdp", "seq", None),
        P(),
        P(("seq", "fsdp"), None),
        P(("seq", "fsdp"), None),
        P(("seq", "fsdp"), None),
        P(None, ("seq", "fsdp")),
    )
    return jax.shard_map(
        body, mesh=mesh, in_specs=placed, out_specs=P("fsdp", "seq", None), check_vma=False
    )
```

profile of v0, /device:TPU:0, one launch (start us, length us, event | category | flops | bytes accessed | tf_op | source)
XLA Modules:
  0.0 635.2 jit_solution(5943152748968882074)
XLA Ops:
  6.5 0.7 all-gather.10.cloned.1.call-update
  7.3 0.7 all-gather.8.cloned.1.call-update
  8.1 0.7 all-gather.6.cloned.1.call-update
  8.8 0.5 fusion.8
  9.3 1.9 fusion.10
  11.2 9.5 %copy.25 = bf16[1,128,8192]{1,0,2:T(2,128)(2,1)} copy(bf16[1,128,8192]{2,1,0:T(8,128)(2,1)} %fusion.10) | data formatting | bytes 4194304 | tf_op jit(solution)/shard_map/convert_element_type | solution.py:12
  20.7 0.6 broadcast.27
  21.3 46.5 %reduce.1 = bf16[8192,128]{1,0:T(8,128)(2,1)} reduce(bf16[8192,1,128]{2,1,0:T(2,128)(2,1)} %bitcast.52, bf16[]{:T(256)} %broadcast.27), dimensions={1}, to_apply=%bitcast.23.reduce_sub_computation | reduce | bytes 4194306
  67.8 4.0 reshape.53
  71.8 31.4 %all_to_all.24 = bf16[4,2,131072]{2,1,0:T(2,128)(2,1)} all-to-all(bf16[4,2,131072]{2,1,0:T(2,128)(2,1)} %reshape.53), channel_id=1, replica_groups=mesh['seq'=4,'fsdp'=8] {'seq'}, dimensions={0} | all-to-all | bytes 4194304 | tf_op jit(solution)/shard_map/all_to_all | solution.py:13
  103.2 4.9 reshape.54
  108.2 3.9 copy.33
  112.0 4.0 copy.26
  116.0 4.3 convolution_convert_fusion.3
  120.3 4.4 convolution_convert_fusion.4
  124.7 0.2 reduce-scatter.2.cloned.1.call-start
  125.0 98.2 %all-gather.6.cloned.1.call-done = bf16[2048,4096]{1,0:T(8,128)(2,1)} async-done(((bf16[256,4096]{1,0:T(8,128)(2,1)}), bf16[2048,4096]{1,0:T(8,128)(2,1)}) %all-gather.6.cloned.1.call-update) | async-done | bytes 16777232 | tf_op jit(solution)/shard_map/all_gather | solution.py:22
  223.1 14.3 %convolution_convert_fusion.1 = bf16[512,4096]{1,0:T(8,128)(2,1)} fusion(bf16[512,2048]{1,0:T(8,128)(2,1)} %bitcast.60, bf16[2048,4096]{1,0:T(8,128)(2,1)} %all-gather.6.cloned.1.call-done), kind=kOutput, calls=%fused_computation.16 | convolution fusion | flops 8592031744 | bytes 23068672 | tf_op jit(solution)/shard_map/dot_general | solution.py:27
  237.5 0.5 all-gather.14.cloned.1.call-update
  238.1 38.6 %all-reduce.3.cloned.1.call-done = (bf16[512,512]{1,0:T(8,128)(2,1)}, bf16[512,512]{1,0:T(8,128)(2,1)}) async-done(((bf16[512,512]{1,0:T(8,128)(2,1)}, bf16[512,512]{1,0:T(8,128)(2,1)}), (bf16[512,512]{1,0:T(8,128)(2,1)}, bf16[512,512]{1,0:T(8,128)(2,1)})) %all-reduce.3.cloned.1.call-update) | async-done | bytes 1048592 | tf_op jit(solution)/shard_map/psum | solution.py:33
  276.8 1.6 convert_convert_fusion
  278.4 53.8 %reduce-scatter.2.cloned.1.call-done = bf16[512,1024]{1,0:T(8,128)(2,1)} async-done(((bf16[512,4096]{1,0:T(8,128)(2,1)}), bf16[512,1024]{1,0:T(8,128)(2,1)}) %reduce-scatter.2.cloned.1.call-update) | async-done | bytes 1048592 | tf_op jit(solution)/shard_map/reduce_scatter | solution.py:29
  332.2 2.4 bitcast_bitcast_fusion
  334.6 16.4 %while.11 = (s32[]{:T(128)}, bf16[8,512,128]{1,2,0:T(8,128)(2,1)S(1)}, bf16[8,512,128]{2,1,0:T(8,128)(2,1)}, bf16[512,128]{1,0:T(8,128)(2,1)}, bf16[512,128]{1,0:T(8,128)(2,1)S(1)}, /*index=5*/s32[]{:T(128)}) while((s32[]{:T(128)}, bf16[8,512,128]{1,2,0:T(8,128)(2,1)S(1)}, bf16[8,512,128]{2,1,0:T(8,128)(2,1)}, ...), condition=%wide.region_7.8_spmd.clone, body=%wide.region_4.7_spmd.clone.sunk | while | flops 136641536 | bytes 4205129 | solution.py:56
  334.6 1.3 fusion.31
  335.8 0.2 fusion.32
  336.0 0.4 fusion.33
  336.6 1.3 fusion.31
  337.9 0.2 fusion.32
  338.1 0.4 fusion.33
  338.5 0.1 copy.41
  338.6 1.3 fusion.31
  339.9 0.2 fusion.32
  340.1 0.4 fusion.33
  340.5 0.1 copy.41
  340.6 1.3 fusion.31
  342.0 0.2 fusion.32
  342.2 0.4 fusion.33
  342.6 0.1 copy.41
  342.7 1.3 fusion.31
  344.0 0.2 fusion.32
  344.2 0.4 fusion.33
  344.8 1.3 fusion.31
  346.1 0.2 fusion.32
  346.3 0.4 fusion.33
  346.7 0.1 copy.41
  346.9 1.3 fusion.31
  348.2 0.2 fusion.32
  348.4 0.4 fusion.33
  348.9 1.3 fusion.31
  350.2 0.2 fusion.32
  350.4 0.4 fusion.33
  350.9 1.0 copy-done.1
  351.9 133.5 %all-gather.14.cloned.1.call-done = bf16[4096,2048]{1,0:T(8,128)(2,1)} async-done(((bf16[4096,256]{1,0:T(8,128)(2,1)}), bf16[4096,2048]{1,0:T(8,128)(2,1)}) %all-gather.14.cloned.1.call-update) | async-done | bytes 16777232 | tf_op jit(solution)/shard_map/all_gather | solution.py:58
  485.5 52.6 %all-gather.12.cloned.1.call-done = bf16[512,4096]{0,1:T(8,128)(2,1)} async-done(((bf16[512,1024]{0,1:T(8,128)(2,1)}), bf16[512,4096]{0,1:T(8,128)(2,1)}) %all-gather.12.cloned.1.call-update) | async-done | bytes 4194320 | tf_op jit(solution)/shard_map/all_gather | solution.py:60
  538.1 13.6 %fusion.11 = bf16[1,512,2048]{2,1,0:T(8,128)(2,1)S(1)} fusion(bf16[512,4096]{0,1:T(8,128)(2,1)} %all-gather.12.cloned.1.call-done, bf16[4096,2048]{1,0:T(8,128)(2,1)} %all-gather.14.cloned.1.call-done), kind=kOutput, calls=%fused_computation.22 | convolution fusion | flops 8590983168 | bytes 23068672 | tf_op jit(solution)/shard_map/dot_general | solution.py:59
  551.7 5.2 copy.39
  557.0 14.5 %reduce.2 = bf16[512,2048]{1,0:T(8,128)(2,1)} reduce(bf16[512,1,2048]{2,1,0:T(2,128)(2,1)} %bitcast.53, bf16[]{:T(256)} %broadcast.27), dimensions={1}, to_apply=%bitcast.43.reduce_sub_computation | reduce | bytes 4194306
  571.5 4.5 reshape.55
  576.0 29.9 %all_to_all.25 = bf16[4,2,131072]{2,1,0:T(2,128)(2,1)} all-to-all(bf16[4,2,131072]{2,1,0:T(2,128)(2,1)} %reshape.55), channel_id=1, replica_groups=mesh['seq'=4,'fsdp'=8] {'seq'}, dimensions={0} | all-to-all | bytes 4194304 | tf_op jit(solution)/shard_map/all_to_all | solution.py:65
  605.9 4.9 reshape.56
  610.9 6.8 %copy.38 = f32[1,4,128,2048]{3,1,2,0:T(4,128)} copy(bf16[1,4,128,2048]{3,0,2,1:T(2,128)(2,1)} %bitcast.55) | data formatting | bytes 6291456 | tf_op jit(solution)/shard_map/convert_element_type | solution.py:66
  617.7 6.0 reshape.51
  623.7 4.6 convert_add_fusion
  (30 shorter events, 0.9 us)
Async XLA Ops:
  6.5 2.3 copy-start
  6.5 109.5 %all-gather.10.cloned.1.call-start = ((), (), s32[]{:S(2)}) async-start(), calls=%async_computation.6 | async-start | bytes 2359296 | tf_op jit(solution)/shard_map/all_gather | solution.py:24
  7.3 113.0 %all-gather.8.cloned.1.call-start = ((), (), s32[]{:S(2)}) async-start(), calls=%async_computation.5 | async-start | bytes 2359296 | tf_op jit(solution)/shard_map/all_gather | solution.py:23
  8.0 1.3 copy-start.2
  8.0 215.1 %all-gather.6.cloned.1.call-start = ((), (), s32[]{:S(2)}) async-start(), calls=%async_computation.3 | async-start | bytes 18874368 | tf_op jit(solution)/shard_map/all_gather | solution.py:22
  8.8 268.0 %all-reduce.3.cloned.1.call-start = ((), (), s32[]{:S(2)}) async-start(), calls=%async_computation.9 | async-start | bytes 2097152 | tf_op jit(solution)/shard_map/psum | solution.py:33
  124.7 207.4 %reduce-scatter.2.cloned.1.call-start = ((), (), s32[]{:S(2)}) async-start(), calls=%async_computation.4 | async-start | bytes 5242880 | tf_op jit(solution)/shard_map/reduce_scatter | solution.py:29
  237.5 248.0 %all-gather.14.cloned.1.call-start = ((), (), s32[]{:S(2)}) async-start(), calls=%async_computation.8 | async-start | bytes 18874368 | tf_op jit(solution)/shard_map/all_gather | solution.py:58
  238.0 300.0 %all-gather.12.cloned.1.call-start = ((), (), s32[]{:S(2)}) async-start(), calls=%async_computation.7 | async-start | bytes 5242880 | tf_op jit(solution)/shard_map/all_gather | solution.py:60
  350.9 1.0 copy-start.1
Sparse Core Ops, SparseCore 0:
  8.9 31.8 all-gather.9
  42.4 28.5 all-gather.7
  72.6 150.4 all-gather.5
  226.0 50.6 all-reduce.2
  279.6 52.5 reduce-scatter.1
  333.6 151.7 all-gather.13
  487.3 50.7 all-gather.11
where the time goes:
time: 636 us; the launch traced here: 635 us
  waiting for transfers between devices  379 us (60%)
  other arithmetic  71.3 us (11%)
  blocking collectives  61.3 us (10%)
  local copies, waits for them, and re-layouts  58.8 us (9%)
  matrix products  50.1 us (8%)
  between operations  13.6 us (2%)
    all_gather x1, waiting for transfers between devices, body(): out_columns = lax.all_gather(w_out, 'fsdp', axis=1, tiled=True)  134 us
    all_gather x1, waiting for transfers between devices, body(): lax.all_gather(w_query, 'fsdp', axis=0, tiled=True)  98.2 us
    unnamed x2, other arithmetic  61.1 us
    reduce_scatter x1, waiting for transfers between devices, body(): lax.psum_scatter(query_part.astype(jnp.bfloat16), 'seq', scatter_dimensio...  53.8 us
    all_gather x1, waiting for transfers between devices, body(): lax.all_gather(heads_out, 'seq', axis=1, tiled=True)  52.6 us
    psum x1, waiting for transfers between devices, body(): lax.psum(key_part.astype(jnp.bfloat16), 'seq').astype(jnp.float32)  38.6 us
    all_to_all x1, blocking collectives, body(): lax.all_to_all(normed_input[None], 'seq', split_axis=2, concat_axis=1, ti...  31.4 us
    all_to_all x1, blocking collectives, body(): lax.all_to_all(branch[None], 'seq', split_axis=1, concat_axis=2, tiled=True)  29.9 us
  transfers between devices with their start and end apart: 7, of which 5 were waited for; matrix products, arithmetic and copies ran while one was open for 19% of the time, Pallas kernels for 0%

commit v1 on v0

--- a/solution.py
+++ b/solution.py
@@ -30,7 +30,7 @@
         query_part.astype(jnp.bfloat16), "seq", scatter_dimension=1, tiled=True
     )
     key_all, value_all = (
-        lax.psum(key_part.astype(jnp.bfloat16), "seq").astype(jnp.float32),
+        jnp.sum(lax.all_gather(key_part.astype(jnp.bfloat16), "seq"), axis=0).astype(jnp.float32),
         lax.psum(value_part.astype(jnp.bfloat16), "seq").astype(jnp.float32),
     )
     offset = device_index * local_heads // group_width * HEAD_SIZE

time: 636 us -> 666 us (1.047)
  waiting for transfers between devices: 379 us -> 406 us
    all_gather x0 -> x1, waiting for transfers between devices: none -> 36 us  [body(): lax.all_gather(key_part.astype(jnp.bfloat16), 'seq')]
    psum x1, waiting for transfers between devices: 38.6 us -> 31.3 us  [body(): lax.psum(value_part.astype(jnp.bfloat16), 'seq').astype(jnp.float32)]
  transfers between devices with their start and end apart: 7 -> 8, of which waited for: 5 -> 6; matrix products, arithmetic and copies ran while one was open for 19% -> 18% of each run, Pallas kernels for 0% -> 0%
where the time goes in v1:
time: 666 us; the launch traced here: 665 us
  waiting for transfers between devices  406 us (61%)
  other arithmetic  74.9 us (11%)
  blocking collectives  61.3 us (9%)
  local copies, waits for them, and re-layouts  58.8 us (9%)
  matrix products  50.1 us (8%)
  between operations  13.6 us (2%)
    all_gather x1, waiting for transfers between devices, body(): out_columns = lax.all_gather(w_out, 'fsdp', axis=1, tiled=True)  134 us
    all_gather x1, waiting for transfers between devices, body(): lax.all_gather(w_query, 'fsdp', axis=0, tiled=True)  98.2 us
    unnamed x2, other arithmetic  61 us
    all_gather x1, waiting for transfers between devices, body(): lax.all_gather(heads_out, 'seq', axis=1, tiled=True)  52.6 us
    reduce_scatter x1, waiting for transfers between devices, body(): lax.psum_scatter(query_part.astype(jnp.bfloat16), 'seq', scatter_dimensio...  51 us
    all_gather x1, waiting for transfers between devices, body(): lax.all_gather(key_part.astype(jnp.bfloat16), 'seq')  36 us
    all_to_all x1, blocking collectives, body(): lax.all_to_all(normed_input[None], 'seq', split_axis=2, concat_axis=1, ti...  31.4 us
    psum x1, waiting for transfers between devices, body(): lax.psum(value_part.astype(jnp.bfloat16), 'seq').astype(jnp.float32)  31.3 us
  transfers between devices with their start and end apart: 8, of which 6 were waited for; matrix products, arithmetic and copies ran while one was open for 18% of the time, Pallas kernels for 0%

profile of v1, /device:TPU:0, one launch (start us, length us, event | category | flops | bytes accessed | tf_op | source)
XLA Modules:
  0.0 665.0 jit_solution(14773272825732324825)
XLA Ops:
  6.5 0.7 all-gather.12.cloned.1.call-update
  7.3 0.7 all-gather.10.cloned.1.call-update
  8.1 0.7 all-gather.8.cloned.1.call-update
  8.8 0.5 fusion.8
  9.3 1.9 fusion.10
  11.2 9.5 %copy.25 = bf16[1,128,8192]{1,0,2:T(2,128)(2,1)} copy(bf16[1,128,8192]{2,1,0:T(8,128)(2,1)} %fusion.10) | data formatting | bytes 4194304 | tf_op jit(solution)/shard_map/convert_element_type | solution.py:12
  20.7 0.5 broadcast.27
  21.3 46.5 %reduce.2 = bf16[8192,128]{1,0:T(8,128)(2,1)} reduce(bf16[8192,1,128]{2,1,0:T(2,128)(2,1)} %bitcast.53, bf16[]{:T(256)} %broadcast.27), dimensions={1}, to_apply=%bitcast.24.reduce_sub_computation | reduce | bytes 4194306
  67.7 4.0 reshape.54
  71.7 31.4 %all_to_all.24 = bf16[4,2,131072]{2,1,0:T(2,128)(2,1)} all-to-all(bf16[4,2,131072]{2,1,0:T(2,128)(2,1)} %reshape.54), channel_id=1, replica_groups=mesh['seq'=4,'fsdp'=8] {'seq'}, dimensions={0} | all-to-all | bytes 4194304 | tf_op jit(solution)/shard_map/all_to_all | solution.py:13
  103.1 4.9 reshape.55
  108.1 3.8 copy.33
  111.9 4.0 copy.26
  115.9 4.3 convolution_convert_fusion.3
  120.3 4.4 convolution_convert_fusion.4
  124.7 0.2 reduce-scatter.2.cloned.1.call-start
  125.0 98.2 %all-gather.8.cloned.1.call-done = bf16[2048,4096]{1,0:T(8,128)(2,1)} async-done(((bf16[256,4096]{1,0:T(8,128)(2,1)}), bf16[2048,4096]{1,0:T(8,128)(2,1)}) %all-gather.8.cloned.1.call-update) | async-done | bytes 16777232 | tf_op jit(solution)/shard_map/all_gather | solution.py:22
  223.1 14.3 %convolution_convert_fusion.1 = bf16[512,4096]{1,0:T(8,128)(2,1)} fusion(bf16[512,2048]{1,0:T(8,128)(2,1)} %bitcast.62, bf16[2048,4096]{1,0:T(8,128)(2,1)} %all-gather.8.cloned.1.call-done), kind=kOutput, calls=%fused_computation.16 | convolution fusion | flops 8592031744 | bytes 23068672 | tf_op jit(solution)/shard_map/dot_general | solution.py:27
  237.5 0.7 all-gather.16.cloned.1.call-update
  238.3 31.3 %all-reduce.2.cloned.1.call-done = bf16[512,512]{1,0:T(8,128)(2,1)} async-done(((bf16[512,512]{1,0:T(8,128)(2,1)}), bf16[512,512]{1,0:T(8,128)(2,1)}) %all-reduce.2.cloned.1.call-update) | async-done | bytes 524304 | tf_op jit(solution)/shard_map/psum | solution.py:34
  269.6 0.9 convert_convert_fusion
  270.5 36.0 %all-gather.18.cloned.1.call-done = bf16[2048,512]{1,0:T(8,128)(2,1)} async-done(((bf16[512,512]{1,0:T(8,128)(2,1)}), bf16[2048,512]{1,0:T(8,128)(2,1)}) %all-gather.18.cloned.1.call-update) | async-done | bytes 2097168 | tf_op jit(solution)/shard_map/all_gather | solution.py:33
  306.5 2.8 reduce_sum.31
  309.3 1.6 convert_convert_fusion.1
  310.9 51.0 %reduce-scatter.2.cloned.1.call-done = bf16[512,1024]{1,0:T(8,128)(2,1)} async-done(((bf16[512,4096]{1,0:T(8,128)(2,1)}), bf16[512,1024]{1,0:T(8,128)(2,1)}) %reduce-scatter.2.cloned.1.call-update) | async-done | bytes 1048592 | tf_op jit(solution)/shard_map/reduce_scatter | solution.py:29
  361.9 2.4 bitcast_bitcast_fusion
  364.3 16.4 %while.11 = (s32[]{:T(128)}, bf16[8,512,128]{1,2,0:T(8,128)(2,1)S(1)}, bf16[8,512,128]{2,1,0:T(8,128)(2,1)}, bf16[512,128]{1,0:T(8,128)(2,1)}, bf16[512,128]{1,0:T(8,128)(2,1)S(1)}, /*index=5*/s32[]{:T(128)}) while((s32[]{:T(128)}, bf16[8,512,128]{1,2,0:T(8,128)(2,1)S(1)}, bf16[8,512,128]{2,1,0:T(8,128)(2,1)}, ...), condition=%wide.region_7.8_spmd.clone, body=%wide.region_4.7_spmd.clone.sunk | while | flops 136641536 | bytes 4205129 | solution.py:56
  364.3 1.3 fusion.31
  365.6 0.2 fusion.32
  365.8 0.4 fusion.33
  366.2 0.1 copy.42
  366.3 1.3 fusion.31
  367.6 0.2 fusion.32
  367.8 0.4 fusion.33
  368.4 1.3 fusion.31
  369.6 0.2 fusion.32
  369.8 0.4 fusion.33
  370.4 1.3 fusion.31
  371.7 0.2 fusion.32
  371.9 0.4 fusion.33
  372.5 1.3 fusion.31
  373.8 0.2 fusion.32
  374.0 0.4 fusion.33
  374.5 1.3 fusion.31
  375.9 0.2 fusion.32
  376.1 0.4 fusion.33
  376.6 1.3 fusion.31
  377.9 0.2 fusion.32
  378.1 0.4 fusion.33
  378.7 1.3 fusion.31
  379.9 0.2 fusion.32
  380.1 0.4 fusion.33
  380.7 1.0 copy-done.1
  381.7 133.6 %all-gather.16.cloned.1.call-done = bf16[4096,2048]{1,0:T(8,128)(2,1)} async-done(((bf16[4096,256]{1,0:T(8,128)(2,1)}), bf16[4096,2048]{1,0:T(8,128)(2,1)}) %all-gather.16.cloned.1.call-update) | async-done | bytes 16777232 | tf_op jit(solution)/shard_map/all_gather | solution.py:58
  515.3 52.6 %all-gather.14.cloned.1.call-done = bf16[512,4096]{0,1:T(8,128)(2,1)} async-done(((bf16[512,1024]{0,1:T(8,128)(2,1)}), bf16[512,4096]{0,1:T(8,128)(2,1)}) %all-gather.14.cloned.1.call-update) | async-done | bytes 4194320 | tf_op jit(solution)/shard_map/all_gather | solution.py:60
  568.0 13.6 %fusion.11 = bf16[1,512,2048]{2,1,0:T(8,128)(2,1)S(1)} fusion(bf16[512,4096]{0,1:T(8,128)(2,1)} %all-gather.14.cloned.1.call-done, bf16[4096,2048]{1,0:T(8,128)(2,1)} %all-gather.16.cloned.1.call-done), kind=kOutput, calls=%fused_computation.22 | convolution fusion | flops 8590983168 | bytes 23068672 | tf_op jit(solution)/shard_map/dot_general | solution.py:59
  581.6 5.2 copy.40
  586.8 14.5 %reduce.3 = bf16[512,2048]{1,0:T(8,128)(2,1)} reduce(bf16[512,1,2048]{2,1,0:T(2,128)(2,1)} %bitcast.54, bf16[]{:T(256)} %broadcast.27), dimensions={1}, to_apply=%bitcast.44.reduce_sub_computation | reduce | bytes 4194306
  601.3 4.5 reshape.56
  605.8 29.9 %all_to_all.25 = bf16[4,2,131072]{2,1,0:T(2,128)(2,1)} all-to-all(bf16[4,2,131072]{2,1,0:T(2,128)(2,1)} %reshape.56), channel_id=1, replica_groups=mesh['seq'=4,'fsdp'=8] {'seq'}, dimensions={0} | all-to-all | bytes 4194304 | tf_op jit(solution)/shard_map/all_to_all | solution.py:65
  635.7 4.9 reshape.57
  640.7 6.8 %copy.39 = f32[1,4,128,2048]{3,1,2,0:T(4,128)} copy(bf16[1,4,128,2048]{3,0,2,1:T(2,128)(2,1)} %bitcast.56) | data formatting | bytes 6291456 | tf_op jit(solution)/shard_map/convert_element_type | solution.py:66
  647.5 6.0 reshape.51
  653.5 4.6 convert_add_fusion
  (35 shorter events, 1.3 us)
Async XLA Ops:
  6.5 2.3 copy-start
  6.5 109.4 %all-gather.12.cloned.1.call-start = ((), (), s32[]{:S(2)}) async-start(), calls=%async_computation.6 | async-start | bytes 2359296 | tf_op jit(solution)/shard_map/all_gather | solution.py:24
  7.3 113.0 %all-gather.10.cloned.1.call-start = ((), (), s32[]{:S(2)}) async-start(), calls=%async_computation.5 | async-start | bytes 2359296 | tf_op jit(solution)/shard_map/all_gather | solution.py:23
  8.0 1.3 copy-start.2
  8.0 215.1 %all-gather.8.cloned.1.call-start = ((), (), s32[]{:S(2)}) async-start(), calls=%async_computation.3 | async-start | bytes 18874368 | tf_op jit(solution)/shard_map/all_gather | solution.py:22
  8.8 260.8 %all-reduce.2.cloned.1.call-start = ((), (), s32[]{:S(2)}) async-start(), calls=%async_computation.7 | async-start | bytes 1048576 | tf_op jit(solution)/shard_map/psum | solution.py:34
  120.2 186.2 %all-gather.18.cloned.1.call-start = ((), (), s32[]{:S(2)}) async-start(), calls=%async_computation.10 | async-start | bytes 2621440 | tf_op jit(solution)/shard_map/all_gather | solution.py:33
  124.7 237.2 %reduce-scatter.2.cloned.1.call-start = ((), (), s32[]{:S(2)}) async-start(), calls=%async_computation.4 | async-start | bytes 5242880 | tf_op jit(solution)/shard_map/reduce_scatter | solution.py:29
  237.5 277.9 %all-gather.16.cloned.1.call-start = ((), (), s32[]{:S(2)}) async-start(), calls=%async_computation.9 | async-start | bytes 18874368 | tf_op jit(solution)/shard_map/all_gather | solution.py:58
  238.2 329.7 %all-gather.14.cloned.1.call-start = ((), (), s32[]{:S(2)}) async-start(), calls=%async_computation.8 | async-start | bytes 5242880 | tf_op jit(solution)/shard_map/all_gather | solution.py:60
  380.7 1.0 copy-start.1
Sparse Core Ops, SparseCore 0:
  8.9 31.8 all-gather.11
  42.4 28.5 all-gather.9
  72.6 150.4 all-gather.7
  226.0 43.5 all-reduce.1
  271.3 35.1 all-gather.17
  309.3 52.5 reduce-scatter.1
  363.5 151.7 all-gather.15
  517.2 50.7 all-gather.13
